TPU v7x, 32 devices: a 4x4x1 block of a 4x4x8 slice. The times are simulated.
32 devices in a mesh: dp: 1 (over z), pz: 4 (over y), py: 4 (over x), px: 2 (over core).
Axes of the slice: x: 4, y: 4, z: 1, core: 2. Of those that a mesh axis runs over, the one named last changes fastest.
The devices are a block of a 4x4x8 slice.
Arguments:
- volumes: bfloat16 [2, 16, 64, 128, 128], P('dp', None, 'px', 'py', 'pz')
- filter_taps: float32 [3, 3, 17], replicated
- mix_weight: bfloat16 [3, 16, 16], replicated
- mix_bias: float32 [3, 16], replicated
Outputs:
- output: bfloat16 [2, 16, 64, 128, 128], P('dp', None, 'px', 'py', 'pz')
All inputs are finite; a program needn't handle non-finite values.
Results may differ from a plain program's by a relative error of at most 0.00376.
Values are sent between devices in bfloat16 or wider.
A program may use at most 768 MiB of HBM per device.

v0:
```python
import jax
import jax.numpy as jnp
from jax import lax
from jax.sharding import PartitionSpec as P

PASS_FORMS = ('vcsyz,si->vciyz', 'vcxsz,si->vcxiz', 'vcxys,si->vcxyi')
GRID_AXES = ((2, 'px'), (3, 'py'), (4, 'pz'))


def band_matrix(tap_row, out_len):
    tap_count = tap_row.shape[0]
    tap_index = jnp.arange(out_len + tap_count - 1)[:, None] - jnp.arange(out_len)[None, :]
    inside = (tap_index >= 0) & (tap_index < tap_count)
    picked = tap_row[jnp.clip(tap_index, 0, tap_count - 1)]
    return jnp.where(inside, picked, 0.0).astype(jnp.bfloat16)


def neighbour_planes(block, plane_count, axis_dim, axis_name, axis_size):
    if axis_size == 1:
        zero_shape = block.shape[:axis_dim] + (plane_count,) + block.shape[axis_dim + 1:]
        zero_planes = jnp.zeros(zero_shape, block.dtype)
        return zero_planes, zero_planes
    extent = block.shape[axis_dim]
    low_planes = lax.slice_in_dim(block, 0, plane_count, axis=axis_dim)
    high_planes = lax.slice_in_dim(block, extent - plane_count, extent, axis=axis_dim)
    upward = [(source, source + 1) for source in range(axis_size - 1)]
    downward = [(source + 1, source) for source in range(axis_size - 1)]
    from_lower = lax.ppermute(high_planes, axis_name, upward)
    from_upper = lax.ppermute(low_planes, axis_name, downward)
    return from_lower, from_upper


def solution(mesh):
    axis_sizes = {'px': mesh.shape['px'], 'py': mesh.shape['py'], 'pz': mesh.shape['pz']}
    vol_spec = P('dp', None, 'px', 'py', 'pz')

    def local_layers(vol_block, filter_taps, mix_weight, mix_bias):
        half_width = (filter_taps.shape[2] - 1) // 2
        vol_state = vol_block
        for layer_idx in range(filter_taps.shape[0]):
            current = vol_state
            for pass_idx in range(3):
                axis_dim, axis_name = GRID_AXES[pass_idx]
                from_lower, from_upper = neighbour_planes(current, half_width, axis_dim, axis_name, axis_sizes[axis_name])
                padded = jnp.concatenate([from_lower, current, from_upper], axis=axis_dim)
                matrix = band_matrix(filter_taps[layer_idx, pass_idx], current.shape[axis_dim])
                current = jnp.einsum(PASS_FORMS[pass_idx], padded, matrix, preferred_element_type=jnp.float32).astype(jnp.bfloat16)
            mix_out = jnp.einsum('cd,vcxyz->vdxyz', mix_weight[layer_idx], current, preferred_element_type=jnp.float32)
            activated = jax.nn.gelu(mix_out + mix_bias[layer_idx][None, :, None, None, None], approximate=True)
            vol_state = (vol_state.astype(jnp.float32) + activated).astype(jnp.bfloat16)
        return vol_state

    return jax.shard_map(local_layers, mesh=mesh, in_specs=(vol_spec, P(), P(), P()), out_specs=vol_spec, check_vma=False)
```

profile of v0, /device:TPU:97, one launch (start us, length us, event | category | flops | bytes accessed | tf_op | source)
XLA Modules:
  0.0 739.0 jit_solution(18443918761353585124)
XLA Ops:
  12.4 14.1 %copy.66 = bf16[2,16,32,32,32]{2,4,3,1,0:T(8,128)(2,1)} copy(bf16[2,16,32,32,32]{4,3,2,1,0:T(8,128)(2,1)} %param.4) | data formatting | bytes 4194304 | tf_op args[0]
  50.5 20.0 %convert_bitcast_fusion.5 = bf16[2,16,32,32,32]{4,2,3,1,0:T(8,128)(2,1)} fusion(bf16[2,16,8,32,32]{2,4,3,1,0:T(8,128)(2,1)} %copy.67, bf16[2,16,32,32,32]{2,4,3,1,0:T(8,128)(2,1)} %copy.66, bf16[2,16,8,32,32]{2,4,3,1,0:T(8,128)(2,1)} %copy.65, bf16[48,32]{0,1:T(8,128)(2,1)S(1)} %copy.64), kind=kOutput, calls=%fused_computation.74 | convolution fusion | flops 111156736 | bytes 5245952 | tf_op jit(solution)/shard_map/vcsyz,si->vciyz/dot_general | solution.py:47
  81.0 9.0 %gather_fusion = bf16[1536]{0:T(1024)(128)(2,1)S(1)} fusion(bf16[17]{0:T(256)(128)(2,1)S(1)} %get-tuple-element.30, s32[2048]{0:T(1024)S(1)} %pad_clamp_fusion), kind=kCustom, calls=%fused_computation | custom fusion | bytes 12288 | tf_op jit(solution)/shard_map/gather | solution.py:14
  90.1 34.3 %collective-permute-done.2 = bf16[2,16,32,8,32]{4,2,3,1,0:T(8,128)(2,1)S(1)} collective-permute-done((bf16[2,16,32,8,32]{4,2,3,1,0:T(8,128)(2,1)}, bf16[2,16,32,8,32]{4,2,3,1,0:T(8,128)(2,1)S(1)}, u32[]{:S(2)}, u32[]{:S(2)}) %collective-permute-start.2) | collective-permute-done | bytes 524320 | tf_op jit(solution)/shard_map/ppermute | solution.py:28
  129.1 14.2 %pad_maximum_fusion = bf16[2,16,32,48,32]{4,2,3,1,0:T(8,128)(2,1)} fusion(bf16[2,16,32,8,32]{4,2,3,1,0:T(8,128)(2,1)} %collective-permute-done.3, bf16[2,16,32,32,32]{4,2,3,1,0:T(8,128)(2,1)} %convert_bitcast_fusion.5, bf16[2,16,32,8,32]{4,2,3,1,0:T(8,128)(2,1)S(1)} %collective-permute-done.2), kind=kLoop, calls=%fused_computation.39 | loop fusion | flops 3145728 | bytes 6291456 | tf_op jit(solution)/shard_map/concatenate | solution.py:45
  143.3 9.7 %convert_bitcast_fusion.4 = bf16[2,16,32,32,32]{3,4,2,1,0:T(8,128)(2,1)S(1)} fusion(bf16[2,16,32,48,32]{4,2,3,1,0:T(8,128)(2,1)} %pad_maximum_fusion, bf16[48,32]{0,1:T(8,128)(2,1)S(1)} %copy.63), kind=kOutput, calls=%fused_computation.73 | convolution fusion | flops 101719552 | bytes 5245952 | tf_op jit(solution)/shard_map/vcxsz,si->vcxiz/dot_general | solution.py:47
  164.8 9.0 %gather_fusion.2 = bf16[1536]{0:T(1024)(128)(2,1)S(1)} fusion(bf16[17]{0:T(256)(128)(2,1)S(1)} %get-tuple-element.28, s32[2048]{0:T(1024)S(1)} %pad_clamp_fusion), kind=kCustom, calls=%fused_computation.2 | custom fusion | bytes 12288 | tf_op jit(solution)/shard_map/gather | solution.py:14
  174.6 33.5 %collective-permute-done.4 = bf16[2,16,32,32,8]{3,4,2,1,0:T(8,128)(2,1)S(1)} collective-permute-done((bf16[2,16,32,32,8]{3,4,2,1,0:T(8,128)(2,1)}, bf16[2,16,32,32,8]{3,4,2,1,0:T(8,128)(2,1)S(1)}, u32[]{:S(2)}, u32[]{:S(2)}) %collective-permute-start.4) | collective-permute-done | bytes 524320 | tf_op jit(solution)/shard_map/ppermute | solution.py:28
  212.7 10.6 %pad_maximum_fusion.1 = bf16[2,16,32,32,48]{3,4,2,1,0:T(8,128)(2,1)} fusion(bf16[2,16,32,32,8]{3,4,2,1,0:T(8,128)(2,1)} %collective-permute-done.5, bf16[2,16,32,32,32]{3,4,2,1,0:T(8,128)(2,1)} %copy-done.2, bf16[2,16,32,32,8]{3,4,2,1,0:T(8,128)(2,1)S(1)} %collective-permute-done.4), kind=kLoop, calls=%fused_computation.40 | loop fusion | flops 9437184 | bytes 6291456 | tf_op jit(solution)/shard_map/concatenate | solution.py:45
  223.3 15.5 %copy.70 = bf16[2,16,32,32,48]{4,1,3,2,0:T(8,128)(2,1)} copy(bf16[2,16,32,32,48]{3,4,2,1,0:T(8,128)(2,1)} %pad_maximum_fusion.1) | data formatting | bytes 6291456 | tf_op jit(solution)/shard_map/concatenate | solution.py:45
  238.8 14.5 %fusion.8 = bf16[2,16,32,32,32]{4,1,3,2,0:T(8,128)(2,1)} fusion(bf16[2,16,32,32,32]{4,3,2,1,0:T(8,128)(2,1)} %param.4, f32[16]{0:T(128)S(1)} %get-tuple-element.33, bf16[2,16,32,32,48]{4,1,3,2,0:T(8,128)(2,1)} %copy.70, bf16[48,32]{0,1:T(8,128)(2,1)S(1)} %copy.69, bf16[3,16,16]{2,1,0:T(8,128)(2,1)S(1)} %copy-done.8), kind=kOutput, calls=%fused_computation.20 | convolution fusion | flops 147856896 | bytes 7352832 | tf_op jit(solution)/shard_map/cd,vcxyz->vdxyz/dot_general | solution.py:48
  273.8 13.2 %pad_maximum_fusion.2 = bf16[2,16,48,32,32]{4,1,3,2,0:T(8,128)(2,1)} fusion(bf16[2,16,8,32,32]{4,1,3,2,0:T(8,128)(2,1)} %collective-permute-done.7, bf16[2,16,32,32,32]{4,1,3,2,0:T(8,128)(2,1)} %fusion.8, bf16[2,16,8,32,32]{4,1,3,2,0:T(8,128)(2,1)S(1)} %collective-permute-done.6), kind=kLoop, calls=%fused_computation.41 | loop fusion | flops 3145728 | bytes 6291456 | tf_op jit(solution)/shard_map/concatenate | solution.py:45
  287.1 24.9 %convert_bitcast_fusion.3 = bf16[2,16,32,32,32]{4,2,3,1,0:T(8,128)(2,1)} fusion(bf16[2,16,48,32,32]{4,1,3,2,0:T(8,128)(2,1)} %pad_maximum_fusion.2, bf16[48,32]{0,1:T(8,128)(2,1)S(1)} %copy.73), kind=kOutput, calls=%fused_computation.70 | convolution fusion | flops 101719552 | bytes 5245952 | tf_op jit(solution)/shard_map/vcsyz,si->vciyz/dot_general | solution.py:47
  322.1 9.0 %gather_fusion.3 = bf16[1536]{0:T(1024)(128)(2,1)S(1)} fusion(bf16[17]{0:T(256)(128)(2,1)S(1)} %get-tuple-element.27, s32[2048]{0:T(1024)S(1)} %pad_clamp_fusion), kind=kCustom, calls=%fused_computation.3 | custom fusion | bytes 12288 | tf_op jit(solution)/shard_map/gather | solution.py:14
  331.2 33.2 %collective-permute-done.8 = bf16[2,16,32,8,32]{4,2,3,1,0:T(8,128)(2,1)S(1)} collective-permute-done((bf16[2,16,32,8,32]{4,2,3,1,0:T(8,128)(2,1)}, bf16[2,16,32,8,32]{4,2,3,1,0:T(8,128)(2,1)S(1)}, u32[]{:S(2)}, u32[]{:S(2)}) %collective-permute-start.8) | collective-permute-done | bytes 524320 | tf_op jit(solution)/shard_map/ppermute | solution.py:28
  368.8 14.2 %pad_maximum_fusion.3 = bf16[2,16,32,48,32]{4,2,3,1,0:T(8,128)(2,1)} fusion(bf16[2,16,32,8,32]{4,2,3,1,0:T(8,128)(2,1)} %collective-permute-done.9, bf16[2,16,32,32,32]{4,2,3,1,0:T(8,128)(2,1)} %convert_bitcast_fusion.3, bf16[2,16,32,8,32]{4,2,3,1,0:T(8,128)(2,1)S(1)} %collective-permute-done.8), kind=kLoop, calls=%fused_computation.42 | loop fusion | flops 3145728 | bytes 6291456 | tf_op jit(solution)/shard_map/concatenate | solution.py:45
  383.0 9.7 %convert_bitcast_fusion.2 = bf16[2,16,32,32,32]{3,4,2,1,0:T(8,128)(2,1)S(1)} fusion(bf16[2,16,32,48,32]{4,2,3,1,0:T(8,128)(2,1)} %pad_maximum_fusion.3, bf16[48,32]{0,1:T(8,128)(2,1)S(1)} %copy.72), kind=kOutput, calls=%fused_computation.69 | convolution fusion | flops 101719552 | bytes 5245952 | tf_op jit(solution)/shard_map/vcxsz,si->vcxiz/dot_general | solution.py:47
  404.1 9.0 %gather_fusion.5 = bf16[1536]{0:T(1024)(128)(2,1)S(1)} fusion(bf16[17]{0:T(256)(128)(2,1)S(1)} %get-tuple-element.25, s32[2048]{0:T(1024)S(1)} %pad_clamp_fusion), kind=kCustom, calls=%fused_computation.5 | custom fusion | bytes 12288 | tf_op jit(solution)/shard_map/gather | solution.py:14
  413.3 34.8 %collective-permute-done.10 = bf16[2,16,32,32,8]{3,4,2,1,0:T(8,128)(2,1)S(1)} collective-permute-done((bf16[2,16,32,32,8]{3,4,2,1,0:T(8,128)(2,1)}, bf16[2,16,32,32,8]{3,4,2,1,0:T(8,128)(2,1)S(1)}, u32[]{:S(2)}, u32[]{:S(2)}) %collective-permute-start.10) | collective-permute-done | bytes 524320 | tf_op jit(solution)/shard_map/ppermute | solution.py:28
  452.3 10.6 %pad_maximum_fusion.4 = bf16[2,16,32,32,48]{3,4,2,1,0:T(8,128)(2,1)} fusion(bf16[2,16,32,32,8]{3,4,2,1,0:T(8,128)(2,1)} %collective-permute-done.11, bf16[2,16,32,32,32]{3,4,2,1,0:T(8,128)(2,1)} %copy-done.4, bf16[2,16,32,32,8]{3,4,2,1,0:T(8,128)(2,1)S(1)} %collective-permute-done.10), kind=kLoop, calls=%fused_computation.43 | loop fusion | flops 9437184 | bytes 6291456 | tf_op jit(solution)/shard_map/concatenate | solution.py:45
  462.9 15.5 %copy.77 = bf16[2,16,32,32,48]{4,1,3,2,0:T(8,128)(2,1)} copy(bf16[2,16,32,32,48]{3,4,2,1,0:T(8,128)(2,1)} %pad_maximum_fusion.4) | data formatting | bytes 6291456 | tf_op jit(solution)/shard_map/concatenate | solution.py:45
  478.4 13.4 %fusion.17 = bf16[2,16,32,32,32]{4,1,3,2,0:T(8,128)(2,1)} fusion(bf16[2,16,32,32,32]{4,1,3,2,0:T(8,128)(2,1)} %fusion.8, f32[16]{0:T(128)S(1)} %get-tuple-element.34, bf16[2,16,32,32,48]{4,1,3,2,0:T(8,128)(2,1)} %copy.77, bf16[48,32]{0,1:T(8,128)(2,1)S(1)} %copy.76, bf16[3,16,16]{2,1,0:T(8,128)(2,1)S(1)} %copy-done.8), kind=kOutput, calls=%fused_computation.29 | convolution fusion | flops 147856896 | bytes 7352832 | tf_op jit(solution)/shard_map/cd,vcxyz->vdxyz/dot_general | solution.py:48
  512.3 13.2 %pad_maximum_fusion.5 = bf16[2,16,48,32,32]{4,1,3,2,0:T(8,128)(2,1)} fusion(bf16[2,16,8,32,32]{4,1,3,2,0:T(8,128)(2,1)} %collective-permute-done.13, bf16[2,16,32,32,32]{4,1,3,2,0:T(8,128)(2,1)} %fusion.17, bf16[2,16,8,32,32]{4,1,3,2,0:T(8,128)(2,1)S(1)} %collective-permute-done.12), kind=kLoop, calls=%fused_computation.44 | loop fusion | flops 3145728 | bytes 6291456 | tf_op jit(solution)/shard_map/concatenate | solution.py:45
  525.5 24.9 %convert_bitcast_fusion.1 = bf16[2,16,32,32,32]{4,2,3,1,0:T(8,128)(2,1)} fusion(bf16[2,16,48,32,32]{4,1,3,2,0:T(8,128)(2,1)} %pad_maximum_fusion.5, bf16[48,32]{0,1:T(8,128)(2,1)S(1)} %copy.80), kind=kOutput, calls=%fused_computation.66 | convolution fusion | flops 101719552 | bytes 5245952 | tf_op jit(solution)/shard_map/vcsyz,si->vciyz/dot_general | solution.py:47
  569.4 33.2 %collective-permute-done.14 = bf16[2,16,32,8,32]{4,2,3,1,0:T(8,128)(2,1)S(1)} collective-permute-done((bf16[2,16,32,8,32]{4,2,3,1,0:T(8,128)(2,1)}, bf16[2,16,32,8,32]{4,2,3,1,0:T(8,128)(2,1)S(1)}, u32[]{:S(2)}, u32[]{:S(2)}) %collective-permute-start.14) | collective-permute-done | bytes 524320 | tf_op jit(solution)/shard_map/ppermute | solution.py:28
  606.9 14.2 %pad_maximum_fusion.6 = bf16[2,16,32,48,32]{4,2,3,1,0:T(8,128)(2,1)} fusion(bf16[2,16,32,8,32]{4,2,3,1,0:T(8,128)(2,1)} %collective-permute-done.15, bf16[2,16,32,32,32]{4,2,3,1,0:T(8,128)(2,1)} %convert_bitcast_fusion.1, bf16[2,16,32,8,32]{4,2,3,1,0:T(8,128)(2,1)S(1)} %collective-permute-done.14), kind=kLoop, calls=%fused_computation.45 | loop fusion | flops 3145728 | bytes 6291456 | tf_op jit(solution)/shard_map/concatenate | solution.py:45
  621.2 9.7 %convert_bitcast_fusion = bf16[2,16,32,32,32]{3,4,2,1,0:T(8,128)(2,1)S(1)} fusion(bf16[2,16,32,48,32]{4,2,3,1,0:T(8,128)(2,1)} %pad_maximum_fusion.6, bf16[48,32]{0,1:T(8,128)(2,1)S(1)} %copy.79), kind=kOutput, calls=%fused_computation.65 | convolution fusion | flops 101719552 | bytes 5245952 | tf_op jit(solution)/shard_map/vcxsz,si->vcxiz/dot_general | solution.py:47
  642.1 9.2 %gather_fusion.8 = bf16[1536]{0:T(1024)(128)(2,1)S(1)} fusion(bf16[17]{0:T(256)(128)(2,1)S(1)} %copy-done, s32[2048]{0:T(1024)S(1)} %pad_clamp_fusion), kind=kCustom, calls=%fused_computation.8 | custom fusion | bytes 12288 | tf_op jit(solution)/shard_map/gather | solution.py:14
  651.5 34.6 %collective-permute-done.16 = bf16[2,16,32,32,8]{3,4,2,1,0:T(8,128)(2,1)S(1)} collective-permute-done((bf16[2,16,32,32,8]{3,4,2,1,0:T(8,128)(2,1)}, bf16[2,16,32,32,8]{3,4,2,1,0:T(8,128)(2,1)S(1)}, u32[]{:S(2)}, u32[]{:S(2)}) %collective-permute-start.16) | collective-permute-done | bytes 524320 | tf_op jit(solution)/shard_map/ppermute | solution.py:28
  690.3 10.6 %pad_maximum_fusion.7 = bf16[2,16,32,32,48]{3,4,2,1,0:T(8,128)(2,1)} fusion(bf16[2,16,32,32,8]{3,4,2,1,0:T(8,128)(2,1)} %collective-permute-done.17, bf16[2,16,32,32,32]{3,4,2,1,0:T(8,128)(2,1)} %copy-done.3, bf16[2,16,32,32,8]{3,4,2,1,0:T(8,128)(2,1)S(1)} %collective-permute-done.16), kind=kLoop, calls=%fused_computation.46 | loop fusion | flops 9437184 | bytes 6291456 | tf_op jit(solution)/shard_map/concatenate | solution.py:45
  700.9 15.5 %copy.84 = bf16[2,16,32,32,48]{4,1,3,2,0:T(8,128)(2,1)} copy(bf16[2,16,32,32,48]{3,4,2,1,0:T(8,128)(2,1)} %pad_maximum_fusion.7) | data formatting | bytes 6291456 | tf_op jit(solution)/shard_map/concatenate | solution.py:45
  716.5 13.4 %fusion.26 = bf16[2,16,32,32,32]{4,1,3,2,0:T(8,128)(2,1)} fusion(bf16[2,16,32,32,32]{4,1,3,2,0:T(8,128)(2,1)} %fusion.17, f32[16]{0:T(128)S(1)} %copy-done.7, bf16[2,16,32,32,48]{4,1,3,2,0:T(8,128)(2,1)} %copy.84, bf16[48,32]{0,1:T(8,128)(2,1)S(1)} %copy.83, bf16[3,16,16]{2,1,0:T(8,128)(2,1)S(1)} %copy-done.8), kind=kOutput, calls=%fused_computation.38 | convolution fusion | flops 147856896 | bytes 7352832 | tf_op jit(solution)/shard_map/cd,vcxyz->vdxyz/dot_general | solution.py:48
  (87 shorter events, 188.0 us)
Async XLA Ops:
  0.0 26.6 %copy-start.5 = (f32[3,3,17]{2,1,0:T(4,128)S(1)}, f32[3,3,17]{2,1,0:T(4,128)}, u32[]{:S(2)}) copy-start(f32[3,3,17]{2,1,0:T(4,128)} %param.5) | copy-start | bytes 1840
  5.6 30.8 %collective-permute-start = (bf16[2,16,8,32,32]{4,3,2,1,0:T(8,128)(2,1)}, bf16[2,16,8,32,32]{4,3,2,1,0:T(8,128)(2,1)}, u32[]{:S(2)}, u32[]{:S(2)}) collective-permute-start(bf16[2,16,8,32,32]{4,3,2,1,0:T(8,128)(2,1)} %get-tuple-element.21), channel_id=1, source_target_pairs={{0,1},{2,3},{4,5},{6,7},{8,9},{10,11},{12,13},{14,15},{16,17},{18,... | collective-permute-start | bytes 1572872 | tf_op jit(solution)/shard_map/ppermute | solution.py:28
  6.9 37.5 %collective-permute-start.1 = (bf16[2,16,8,32,32]{4,3,2,1,0:T(8,128)(2,1)}, bf16[2,16,8,32,32]{4,3,2,1,0:T(8,128)(2,1)S(1)}, u32[]{:S(2)}, u32[]{:S(2)}) collective-permute-start(bf16[2,16,8,32,32]{4,3,2,1,0:T(8,128)(2,1)} %get-tuple-element.22), channel_id=1, source_target_pairs={{1,0},{3,2},{5,4},{7,6},{9,8},{11,10},{13,12},{15,14},{17,16},{19,... | collective-permute-start | bytes 1572872 | tf_op jit(solution)/shard_map/ppermute | solution.py:29
  76.1 48.3 %collective-permute-start.2 = (bf16[2,16,32,8,32]{4,2,3,1,0:T(8,128)(2,1)}, bf16[2,16,32,8,32]{4,2,3,1,0:T(8,128)(2,1)S(1)}, u32[]{:S(2)}, u32[]{:S(2)}) collective-permute-start(bf16[2,16,32,8,32]{4,2,3,1,0:T(8,128)(2,1)} %get-tuple-element.19), channel_id=1, source_target_pairs={{0,2},{2,4},{4,6},{1,3},{3,5},{5,7},{8,10},{10,12},{12,14},{9,11},... | collective-permute-start | bytes 1572872 | tf_op jit(solution)/shard_map/ppermute | solution.py:28
  79.5 49.6 %collective-permute-start.3 = (bf16[2,16,32,8,32]{4,2,3,1,0:T(8,128)(2,1)}, bf16[2,16,32,8,32]{4,2,3,1,0:T(8,128)(2,1)}, u32[]{:S(2)}, u32[]{:S(2)}) collective-permute-start(bf16[2,16,32,8,32]{4,2,3,1,0:T(8,128)(2,1)} %get-tuple-element.20), channel_id=1, source_target_pairs={{2,0},{4,2},{6,4},{3,1},{5,3},{7,5},{10,8},{12,10},{14,12},{11,9},... | collective-permute-start | bytes 1572872 | tf_op jit(solution)/shard_map/ppermute | solution.py:29
  153.0 3.4 copy-start.2
  156.4 17.6 %copy-start.6 = (f32[3,16]{1,0:T(4,128)S(1)}, f32[3,16]{1,0:T(4,128)}, u32[]{:S(2)}) copy-start(f32[3,16]{1,0:T(4,128)} %param.7) | copy-start | bytes 580
  159.6 48.4 %collective-permute-start.4 = (bf16[2,16,32,32,8]{3,4,2,1,0:T(8,128)(2,1)}, bf16[2,16,32,32,8]{3,4,2,1,0:T(8,128)(2,1)S(1)}, u32[]{:S(2)}, u32[]{:S(2)}) collective-permute-start(bf16[2,16,32,32,8]{3,4,2,1,0:T(8,128)(2,1)} %get-tuple-element.17), channel_id=1, source_target_pairs={{0,8},{8,16},{16,24},{1,9},{9,17},{17,25},{2,10},{10,18},{18,26},{... | collective-permute-start | bytes 1572872 | tf_op jit(solution)/shard_map/ppermute | solution.py:28
  163.5 49.2 %collective-permute-start.5 = (bf16[2,16,32,32,8]{3,4,2,1,0:T(8,128)(2,1)}, bf16[2,16,32,32,8]{3,4,2,1,0:T(8,128)(2,1)}, u32[]{:S(2)}, u32[]{:S(2)}) collective-permute-start(bf16[2,16,32,32,8]{3,4,2,1,0:T(8,128)(2,1)} %get-tuple-element.18), channel_id=1, source_target_pairs={{8,0},{16,8},{24,16},{9,1},{17,9},{25,17},{10,2},{18,10},{26,18},{... | collective-permute-start | bytes 1572872 | tf_op jit(solution)/shard_map/ppermute | solution.py:29
  223.3 15.5 %copy-start.8 = (bf16[3,16,16]{2,1,0:T(8,128)(2,1)S(1)}, bf16[3,16,16]{2,1,0:T(8,128)(2,1)}, u32[]{:S(2)}) copy-start(bf16[3,16,16]{2,1,0:T(8,128)(2,1)} %param.6) | copy-start | bytes 4612
  258.8 15.1 %collective-permute-start.6 = (bf16[2,16,8,32,32]{4,1,3,2,0:T(8,128)(2,1)}, bf16[2,16,8,32,32]{4,1,3,2,0:T(8,128)(2,1)S(1)}, u32[]{:S(2)}, u32[]{:S(2)}) collective-permute-start(bf16[2,16,8,32,32]{4,1,3,2,0:T(8,128)(2,1)} %get-tuple-element.15), channel_id=1, source_target_pairs={{0,1},{2,3},{4,5},{6,7},{8,9},{10,11},{12,13},{14,15},{16,17},{18,... | collective-permute-start | bytes 1572872 | tf_op jit(solution)/shard_map/ppermute | solution.py:28
  260.1 13.8 %collective-permute-start.7 = (bf16[2,16,8,32,32]{4,1,3,2,0:T(8,128)(2,1)}, bf16[2,16,8,32,32]{4,1,3,2,0:T(8,128)(2,1)}, u32[]{:S(2)}, u32[]{:S(2)}) collective-permute-start(bf16[2,16,8,32,32]{4,1,3,2,0:T(8,128)(2,1)} %get-tuple-element.16), channel_id=1, source_target_pairs={{1,0},{3,2},{5,4},{7,6},{9,8},{11,10},{13,12},{15,14},{17,16},{19,... | collective-permute-start | bytes 1572872 | tf_op jit(solution)/shard_map/ppermute | solution.py:29
  317.5 47.0 %collective-permute-start.8 = (bf16[2,16,32,8,32]{4,2,3,1,0:T(8,128)(2,1)}, bf16[2,16,32,8,32]{4,2,3,1,0:T(8,128)(2,1)S(1)}, u32[]{:S(2)}, u32[]{:S(2)}) collective-permute-start(bf16[2,16,32,8,32]{4,2,3,1,0:T(8,128)(2,1)} %get-tuple-element.13), channel_id=1, source_target_pairs={{0,2},{2,4},{4,6},{1,3},{3,5},{5,7},{8,10},{10,12},{12,14},{9,11},... | collective-permute-start | bytes 1572872 | tf_op jit(solution)/shard_map/ppermute | solution.py:28
  320.7 48.0 %collective-permute-start.9 = (bf16[2,16,32,8,32]{4,2,3,1,0:T(8,128)(2,1)}, bf16[2,16,32,8,32]{4,2,3,1,0:T(8,128)(2,1)}, u32[]{:S(2)}, u32[]{:S(2)}) collective-permute-start(bf16[2,16,32,8,32]{4,2,3,1,0:T(8,128)(2,1)} %get-tuple-element.14), channel_id=1, source_target_pairs={{2,0},{4,2},{6,4},{3,1},{5,3},{7,5},{10,8},{12,10},{14,12},{11,9},... | collective-permute-start | bytes 1572872 | tf_op jit(solution)/shard_map/ppermute | solution.py:29
  392.7 3.4 copy-start.4
  399.3 48.8 %collective-permute-start.10 = (bf16[2,16,32,32,8]{3,4,2,1,0:T(8,128)(2,1)}, bf16[2,16,32,32,8]{3,4,2,1,0:T(8,128)(2,1)S(1)}, u32[]{:S(2)}, u32[]{:S(2)}) collective-permute-start(bf16[2,16,32,32,8]{3,4,2,1,0:T(8,128)(2,1)} %get-tuple-element.11), channel_id=1, source_target_pairs={{0,8},{8,16},{16,24},{1,9},{9,17},{17,25},{2,10},{10,18},{18,26},{... | collective-permute-start | bytes 1572872 | tf_op jit(solution)/shard_map/ppermute | solution.py:28
  402.8 49.5 %collective-permute-start.11 = (bf16[2,16,32,32,8]{3,4,2,1,0:T(8,128)(2,1)}, bf16[2,16,32,32,8]{3,4,2,1,0:T(8,128)(2,1)}, u32[]{:S(2)}, u32[]{:S(2)}) collective-permute-start(bf16[2,16,32,32,8]{3,4,2,1,0:T(8,128)(2,1)} %get-tuple-element.12), channel_id=1, source_target_pairs={{8,0},{16,8},{24,16},{9,1},{17,9},{25,17},{10,2},{18,10},{26,18},{... | collective-permute-start | bytes 1572872 | tf_op jit(solution)/shard_map/ppermute | solution.py:29
  497.2 15.1 %collective-permute-start.12 = (bf16[2,16,8,32,32]{4,1,3,2,0:T(8,128)(2,1)}, bf16[2,16,8,32,32]{4,1,3,2,0:T(8,128)(2,1)S(1)}, u32[]{:S(2)}, u32[]{:S(2)}) collective-permute-start(bf16[2,16,8,32,32]{4,1,3,2,0:T(8,128)(2,1)} %get-tuple-element.9), channel_id=1, source_target_pairs={{0,1},{2,3},{4,5},{6,7},{8,9},{10,11},{12,13},{14,15},{16,17},{18,... | collective-permute-start | bytes 1572872 | tf_op jit(solution)/shard_map/ppermute | solution.py:28
  498.5 13.8 %collective-permute-start.13 = (bf16[2,16,8,32,32]{4,1,3,2,0:T(8,128)(2,1)}, bf16[2,16,8,32,32]{4,1,3,2,0:T(8,128)(2,1)}, u32[]{:S(2)}, u32[]{:S(2)}) collective-permute-start(bf16[2,16,8,32,32]{4,1,3,2,0:T(8,128)(2,1)} %get-tuple-element.10), channel_id=1, source_target_pairs={{1,0},{3,2},{5,4},{7,6},{9,8},{11,10},{13,12},{15,14},{17,16},{19,... | collective-permute-start | bytes 1572872 | tf_op jit(solution)/shard_map/ppermute | solution.py:29
  525.5 34.7 %copy-start.1 = (bf16[17]{0:T(256)(128)(2,1)S(1)}, bf16[17]{0:T(256)(128)(2,1)}, u32[]{:S(2)}) copy-start(bf16[17]{0:T(256)(128)(2,1)} %get-tuple-element.24) | copy-start | bytes 106
  555.9 46.7 %collective-permute-start.14 = (bf16[2,16,32,8,32]{4,2,3,1,0:T(8,128)(2,1)}, bf16[2,16,32,8,32]{4,2,3,1,0:T(8,128)(2,1)S(1)}, u32[]{:S(2)}, u32[]{:S(2)}) collective-permute-start(bf16[2,16,32,8,32]{4,2,3,1,0:T(8,128)(2,1)} %get-tuple-element.7), channel_id=1, source_target_pairs={{0,2},{2,4},{4,6},{1,3},{3,5},{5,7},{8,10},{10,12},{12,14},{9,11},... | collective-permute-start | bytes 1572872 | tf_op jit(solution)/shard_map/ppermute | solution.py:28
  558.9 48.0 %collective-permute-start.15 = (bf16[2,16,32,8,32]{4,2,3,1,0:T(8,128)(2,1)}, bf16[2,16,32,8,32]{4,2,3,1,0:T(8,128)(2,1)}, u32[]{:S(2)}, u32[]{:S(2)}) collective-permute-start(bf16[2,16,32,8,32]{4,2,3,1,0:T(8,128)(2,1)} %get-tuple-element.8), channel_id=1, source_target_pairs={{2,0},{4,2},{6,4},{3,1},{5,3},{7,5},{10,8},{12,10},{14,12},{11,9},... | collective-permute-start | bytes 1572872 | tf_op jit(solution)/shard_map/ppermute | solution.py:29
  621.2 21.0 %copy-start = (bf16[17]{0:T(256)(128)(2,1)S(1)}, bf16[17]{0:T(256)(128)(2,1)}, u32[]{:S(2)}) copy-start(bf16[17]{0:T(256)(128)(2,1)} %get-tuple-element.23) | copy-start | bytes 106
  630.9 3.4 copy-start.3
  637.4 48.7 %collective-permute-start.16 = (bf16[2,16,32,32,8]{3,4,2,1,0:T(8,128)(2,1)}, bf16[2,16,32,32,8]{3,4,2,1,0:T(8,128)(2,1)S(1)}, u32[]{:S(2)}, u32[]{:S(2)}) collective-permute-start(bf16[2,16,32,32,8]{3,4,2,1,0:T(8,128)(2,1)} %get-tuple-element.5), channel_id=1, source_target_pairs={{0,8},{8,16},{16,24},{1,9},{9,17},{17,25},{2,10},{10,18},{18,26},{... | collective-permute-start | bytes 1572872 | tf_op jit(solution)/shard_map/ppermute | solution.py:28
  640.8 49.5 %collective-permute-start.17 = (bf16[2,16,32,32,8]{3,4,2,1,0:T(8,128)(2,1)}, bf16[2,16,32,32,8]{3,4,2,1,0:T(8,128)(2,1)}, u32[]{:S(2)}, u32[]{:S(2)}) collective-permute-start(bf16[2,16,32,32,8]{3,4,2,1,0:T(8,128)(2,1)} %get-tuple-element.6), channel_id=1, source_target_pairs={{8,0},{16,8},{24,16},{9,1},{17,9},{25,17},{10,2},{18,10},{26,18},{... | collective-permute-start | bytes 1572872 | tf_op jit(solution)/shard_map/ppermute | solution.py:29
  700.9 15.5 %copy-start.7 = (f32[16]{0:T(128)S(1)}, f32[16]{0:T(128)}, u32[]{:S(2)}) copy-start(f32[16]{0:T(128)} %get-tuple-element.32) | copy-start | bytes 196
where the time goes:
time: 749 us; the launch traced here: 739 us
  waiting for transfers between devices  230 us (31%)
  local copies, waits for them, and re-layouts  221 us (30%)
  matrix products  140 us (19%)
  other arithmetic  101 us (13%)
  starting transfers between devices  46.9 us (6%)
    ppermute x9, waiting for transfers between devices, neighbour_planes(): from_lower = lax.ppermute(high_planes, axis_name, upward)  204 us
    concatenate x8, other arithmetic, local_layers(): padded = jnp.concatenate([from_lower, current, from_upper], axis=axis_dim)  101 us
    dot_general x6, matrix products, local_layers(): jnp.einsum(PASS_FORMS[pass_idx], padded, matrix, preferred_element_type=j...  98.6 us
    gather x27, local copies, waits for them, and re-layouts, band_matrix(): picked = tap_row[jnp.clip(tap_index, 0, tap_count - 1)]  82.7 us
    concatenate x3, local copies, waits for them, and re-layouts, local_layers(): padded = jnp.concatenate([from_lower, current, from_upper], axis=axis_dim)  46.6 us
    slice x9, local copies, waits for them, and re-layouts, neighbour_planes(): lax.slice_in_dim(block, extent - plane_count, extent, axis=axis_dim)  42.7 us
    dot_general x3, matrix products, local_layers(): jnp.einsum('cd,vcxyz->vdxyz', mix_weight[layer_idx], current, preferred_e...  41.3 us
    ppermute x9, waiting for transfers between devices, neighbour_planes(): from_upper = lax.ppermute(low_planes, axis_name, downward)  26.3 us
  transfers between devices with their start and end apart: 18, of which 12 were waited for; matrix products, arithmetic and copies ran while one was open for 14% of the time, Pallas kernels for 0%

commit v1 on v0

v1 whole, which is shorter than its diff:
```python
import functools
import math

import jax
import jax.numpy as jnp
from jax import lax
from jax.experimental import pallas as pl
from jax.experimental.pallas import tpu as pltpu
from jax.sharding import PartitionSpec as P

MESH = pl.DeviceIdType.MESH
F32 = jnp.float32
BF16 = jnp.bfloat16
LAG_B = 3
LAG_C = 6


def dot(a, b):
    return jnp.dot(a, b, preferred_element_type=F32)


def iota2(shape, dim):
    return lax.broadcasted_iota(jnp.int32, shape, dim)


def kernel(cfg, x_hbm, taps, wt, bias, out_hbm, stage, vb, u1, u2, ob, jsend, jlo, jhi, ksend, klo, khi,
           mi, mj, mjh, mk, mkh, mw, ms, bcol, in_sem, out_sem, xs_sem, xr_sem, js_sem, jr_sem, ks_sem, kr_sem):
    layers, vols, nq, chans, ext, h, ktaps, ny, nz = cfg
    per_layer = vols * nq
    total = layers * per_layer
    px, py, pz = lax.axis_index("px"), lax.axis_index("py"), lax.axis_index("pz")
    mate = 1 - px
    y_lo, y_hi, z_lo, z_hi = py > 0, py < ny - 1, pz > 0, pz < nz - 1

    def place(q):
        return px * q + (1 - px) * (nq - 1 - q)

    def in_copy(c):
        v, q = c // nq, c % nq
        return pltpu.make_async_copy(x_hbm.at[v, :, pl.ds(place(q) * h, h)], stage.at[c], in_sem.at[c])

    for c in range(per_layer):
        in_copy(c).start()

    barrier = pltpu.get_barrier_semaphore()
    pl.semaphore_signal(barrier, inc=1, device_id={"px": mate}, device_id_type=MESH)
    for cond, name, other in ((y_lo, "py", py - 1), (y_hi, "py", py + 1), (z_lo, "pz", pz - 1), (z_hi, "pz", pz + 1)):
        @pl.when(cond)
        def _(name=name, other=other):
            pl.semaphore_signal(barrier, inc=1, device_id={name: other}, device_id_type=MESH)

    lanes = iota2((ext, 256), 1)
    rows = iota2((ext, 256), 0)

    def banded(layer, axis, diff):
        acc = jnp.zeros(diff.shape, F32)
        base = (layer * 3 + axis) * ktaps
        for t in range(ktaps):
            acc = jnp.where(diff == t, taps[base + t], acc)
        return acc

    for q in range(2):
        dirn, hh, i8, kk = lanes // 128, (lanes // 64) % 2, (lanes // h) % 8, lanes % h
        for g in range(8):
            hit = (hh == q) & (i8 == g) & (rows == kk + (ext - h) * dirn)
            ms[q, pl.ds(g * ext, ext), :] = jnp.where(hit, 1.0, 0.0).astype(BF16)

    def build(layer, _):
        lane_i, lane_k = lanes // ext, lanes % ext
        for i_in in range(3 * h):
            val = banded(layer, 0, i_in - lane_i[:8, :])
            full = jnp.concatenate([val] * (ext // 8), axis=0)
            mi[layer, pl.ds(i_in * ext, ext), :] = jnp.where(lane_k == rows, full, 0.0).astype(BF16)
        tj = banded(layer, 1, lane_k - rows + h)
        tk = banded(layer, 2, rows - lane_k + h)
        for g in range(8):
            mj[layer, pl.ds(g * ext, ext), :] = jnp.where(lane_i == g, tj, 0.0).astype(BF16)
            mk[layer, pl.ds(g * ext, ext), :] = jnp.where(lane_i == g, tk, 0.0).astype(BF16)
        l2, r2 = lanes[:, :128], rows[:, :128]
        d2, c2, jj = l2 // 64, (l2 // h) % 8, l2 % h
        tjh = banded(layer, 1, jj + d2 * (ext + h) - r2)
        for g in range(8):
            mjh[layer, pl.ds(g * ext, ext), :] = jnp.where(c2 == g, tjh, 0.0).astype(BF16)
        l3, r3 = lanes[:16, :], rows[:16, :]
        zero = jnp.zeros((64, 256), BF16)
        for d in range(2):
            tkh = banded(layer, 2, r3 % h + d * (ext + h) - l3 % ext)
            for half in range(2):
                mkh[layer, 1 - half, pl.ds(d * 128 + half * 64, 64), :] = zero
                for g in range(0, 8, 2):
                    part = jnp.where(l3 // ext == g + r3 // h, tkh, 0.0).astype(BF16)
                    mkh[layer, half, pl.ds(d * 128 + half * 64 + g * h, 16), :] = part
        r4, l4 = iota2((256, 16), 0), iota2((256, 16), 1)
        e_rows = jnp.where(r4 // 16 == l4, 1.0, 0.0).astype(BF16)
        r5, l5 = iota2((16, 256), 0), iota2((16, 256), 1)
        e_cols = jnp.where(l5 // 16 == r5, 1.0, 0.0).astype(BF16)
        wide = dot(dot(e_rows, wt[layer]).astype(BF16), e_cols)
        rw, lw = iota2((256, 256), 0), iota2((256, 256), 1)
        mw[layer] = jnp.where(rw % 16 == lw % 16, wide, 0.0).astype(BF16)
        bcol[layer] = jnp.broadcast_to(bias[layer], (256, 128))
        return 0

    lax.fori_loop(0, layers, build, 0)

    edge_slot = (1 - px) * 0 + px * (nq + 1)
    big_zero = jnp.zeros((512, 256), BF16)
    for l in range(layers):
        for v in range(vols):
            vb[l, v, edge_slot] = big_zero
    jlo[total] = jnp.zeros((128, 256), BF16)
    jhi[total] = jnp.zeros((128, 256), BF16)
    klo[total] = jnp.zeros((256, 128), BF16)
    khi[total] = jnp.zeros((256, 128), BF16)

    n_wait = 1 + (py > 0).astype(jnp.int32) + (py < ny - 1).astype(jnp.int32) + (pz > 0).astype(jnp.int32) + (pz < nz - 1).astype(jnp.int32)
    pl.semaphore_wait(barrier, n_wait)

    def x_copy(l, v):
        src = px * 1 + (1 - px) * nq
        dst = px * (nq + 1)
        return pltpu.make_async_remote_copy(vb.at[l, v, src], vb.at[l, v, dst], xs_sem.at[l, v], xr_sem.at[l, v],
                                            device_id={"px": mate}, device_id_type=MESH)

    def j_copies(n):
        return (
            (y_hi, y_lo, pltpu.make_async_remote_copy(jsend.at[n, 1], jlo.at[n], js_sem.at[n, 1], jr_sem.at[n, 0],
                                                      device_id={"py": py + 1}, device_id_type=MESH)),
            (y_lo, y_hi, pltpu.make_async_remote_copy(jsend.at[n, 0], jhi.at[n], js_sem.at[n, 0], jr_sem.at[n, 1],
                                                      device_id={"py": py - 1}, device_id_type=MESH)),
        )

    def k_copies(n):
        return (
            (z_hi, z_lo, pltpu.make_async_remote_copy(ksend.at[n, 1], klo.at[n], ks_sem.at[n, 1], kr_sem.at[n, 0],
                                                      device_id={"pz": pz + 1}, device_id_type=MESH)),
            (z_lo, z_hi, pltpu.make_async_remote_copy(ksend.at[n, 0], khi.at[n], ks_sem.at[n, 0], kr_sem.at[n, 1],
                                                      device_id={"pz": pz - 1}, device_id_type=MESH)),
        )

    def convert(c):
        v, q = c // nq, c % nq
        in_copy(c).wait()
        parts = [stage[c, :, a].reshape(chans * ext, ext) for a in range(h)]
        vb[0, v, place(q) + 1] = jnp.concatenate(parts, axis=1)

        @pl.when(q == 0)
        def _():
            x_copy(0, v).start()

    def index(n):
        return n // per_layer, (n // nq) % vols, n % nq

    def stage_a(n):
        l, v, q = index(n)

        @pl.when(q == 0)
        def _():
            x_copy(l, v).wait_recv()

        s = place(q) + 1
        acc = dot(vb[l, v, s - 1], mi[l, 0:256]) + dot(vb[l, v, s], mi[l, 256:512]) + dot(vb[l, v, s + 1], mi[l, 512:768])
        u1[n % 8] = acc.astype(BF16)
        cut = acc.reshape(chans, ext // h, h, 256)
        jsend[n, 0] = cut[:, 0].reshape(chans * h, 256).astype(BF16)
        jsend[n, 1] = cut[:, ext // h - 1].reshape(chans * h, 256).astype(BF16)
        for there, _, copy in j_copies(n):
            pl.when(there)(copy.start)

    def stage_b(n):
        l, v, q = index(n)
        for _, here, copy in j_copies(n):
            pl.when(here)(copy.wait_recv)
        n_lo = jnp.where(y_lo, n, total)
        n_hi = jnp.where(y_hi, n, total)
        packed = None
        for half in range(2):
            main = u1[n % 8, pl.ds(half * 256, 256), :]
            halo = jnp.concatenate([jlo[n_lo, pl.ds(half * 64, 64), :], jhi[n_hi, pl.ds(half * 64, 64), :]], axis=0)
            acc = (dot(mj[l], main) + dot(mjh[l], halo)).astype(BF16)
            u2[n % 8, pl.ds(half * 256, 256), :] = acc
            term = dot(acc, ms[half])
            packed = term if packed is None else packed + term
        packed = packed.astype(BF16)
        ksend[n, 0] = packed[:, :128]
        ksend[n, 1] = packed[:, 128:]
        for there, _, copy in k_copies(n):
            pl.when(there)(copy.start)

    def stage_c(n):
        l, v, q = index(n)
        for _, here, copy in k_copies(n):
            pl.when(here)(copy.wait_recv)
        n_lo = jnp.where(z_lo, n, total)
        n_hi = jnp.where(z_hi, n, total)
        halo = jnp.concatenate([klo[n_lo], khi[n_hi]], axis=1)
        u3 = []
        for half in range(2):
            acc = dot(u2[n % 8, pl.ds(half * 256, 256), :], mk[l]) + dot(halo, mkh[l, half])
            u3.append(acc.astype(BF16).reshape(8, 2, 16, 256))
        s = place(q) + 1
        old = vb[l, v, s].reshape(chans, 2, 16, 256)
        b128 = bcol[l]
        shift = jnp.concatenate([b128, b128], axis=1)
        new = []
        for jh in range(2):
            rhs = jnp.concatenate([u3[0][:, jh].reshape(128, 256), u3[1][:, jh].reshape(128, 256)], axis=0)
            z = dot(mw[l], rhs) + shift
            inner = z * (math.sqrt(2.0 / math.pi) + (0.044715 * math.sqrt(2.0 / math.pi)) * (z * z))
            half_z = 0.5 * z
            act = half_z + half_z * jnp.tanh(inner)
            res = old[:, jh].reshape(256, 256).astype(F32) + act
            new.append(res.astype(BF16).reshape(chans, 1, 16, 256))
        result = jnp.concatenate(new, axis=1).reshape(512, 256)

        @pl.when(l < layers - 1)
        def _():
            vb[l + 1, v, s] = result

            @pl.when(q == 0)
            def _():
                x_copy(l + 1, v).start()

        @pl.when(l == layers - 1)
        def _():
            c = v * nq + q
            ob[c] = result
            out_copy(v, q).start()

    def out_copy(v, q):
        c = v * nq + q
        return pltpu.make_async_copy(ob.at[c], out_hbm.at[v, place(q)], out_sem.at[c])

    convert(0)
    convert(1)

    def tick(t, _):
        @pl.when(t + 2 < per_layer)
        def _():
            convert(t + 2)

        @pl.when(t >= LAG_C)
        def _():
            stage_c(t - LAG_C)

        @pl.when((t >= LAG_B) & (t < total + LAG_B))
        def _():
            stage_b(t - LAG_B)

        @pl.when(t < total)
        def _():
            stage_a(t)
        return 0

    lax.fori_loop(0, total + LAG_C, tick, 0)

    def drain(n, _):
        for there, _, copy in j_copies(n) + k_copies(n):
            pl.when(there)(copy.wait_send)
        return 0

    lax.fori_loop(0, total, drain, 0)
    for l in range(layers):
        for v in range(vols):
            x_copy(l, v).wait_send()
    for v in range(vols):
        for q in range(nq):
            out_copy(v, q).wait()


def unpack_kernel(x_ref, o_ref):
    chans, h, ext = o_ref.shape[1:4]
    for a in range(h):
        o_ref[0, :, a] = x_ref[0, 0, :, a * ext:(a + 1) * ext].reshape(chans, ext, ext)


def solution(mesh):
    ny, nz = mesh.shape["py"], mesh.shape["pz"]
    spec = P("dp", None, "px", "py", "pz")

    def local(x, filter_taps, mix_weight, mix_bias):
        vols, chans, ext = x.shape[0], x.shape[1], x.shape[2]
        layers, ktaps = filter_taps.shape[0], filter_taps.shape[2]
        h = (ktaps - 1) // 2
        nq = ext // h
        total = layers * vols * nq
        cfg = (layers, vols, nq, chans, ext, h, ktaps, ny, nz)
        wt = jnp.swapaxes(mix_weight, 1, 2)
        bias = jnp.repeat(mix_bias, 16, axis=1)[:, :, None]
        vmem = functools.partial(pltpu.VMEM, dtype=BF16)
        dense = pl.pallas_call(
            functools.partial(kernel, cfg),
            out_shape=jax.ShapeDtypeStruct((vols, nq, 512, 256), BF16),
            in_specs=[
                pl.BlockSpec(memory_space=pl.ANY),
                pl.BlockSpec(memory_space=pltpu.SMEM),
                pl.BlockSpec(memory_space=pltpu.VMEM),
                pl.BlockSpec(memory_space=pltpu.VMEM),
            ],
            out_specs=pl.BlockSpec(memory_space=pl.ANY),
            scratch_shapes=[
                pltpu.VMEM((vols * nq, chans, h, ext, ext), BF16),
                pltpu.VMEM((layers, vols, nq + 2, 512, 256), BF16),
                pltpu.VMEM((8, 512, 256), BF16),
                pltpu.VMEM((8, 512, 256), BF16),
                pltpu.VMEM((vols * nq, 512, 256), BF16),
                pltpu.VMEM((total, 2, 128, 256), BF16),
                pltpu.VMEM((total + 1, 128, 256), BF16),
                pltpu.VMEM((total + 1, 128, 256), BF16),
                pltpu.VMEM((total, 2, 256, 128), BF16),
                pltpu.VMEM((total + 1, 256, 128), BF16),
                pltpu.VMEM((total + 1, 256, 128), BF16),
                pltpu.VMEM((layers, 768, 256), BF16),
                pltpu.VMEM((layers, 256, 256), BF16),
                pltpu.VMEM((layers, 256, 128), BF16),
                pltpu.VMEM((layers, 256, 256), BF16),
                pltpu.VMEM((layers, 2, 256, 256), BF16),
                pltpu.VMEM((layers, 256, 256), BF16),
                pltpu.VMEM((2, 256, 256), BF16),
                pltpu.VMEM((layers, 256, 128), F32),
                pltpu.SemaphoreType.DMA((vols * nq,)),
                pltpu.SemaphoreType.DMA((vols * nq,)),
                pltpu.SemaphoreType.DMA((layers, vols)),
                pltpu.SemaphoreType.DMA((layers, vols)),
                pltpu.SemaphoreType.DMA((total, 2)),
                pltpu.SemaphoreType.DMA((total, 2)),
                pltpu.SemaphoreType.DMA((total, 2)),
                pltpu.SemaphoreType.DMA((total, 2)),
            ],
            compiler_params=pltpu.CompilerParams(collective_id=0, has_side_effects=True, vmem_limit_bytes=62 * 1024 * 1024),
            name="layers",
        )(x, filter_taps.reshape(-1), wt, bias)
        return pl.pallas_call(
            unpack_kernel,
            grid=(vols, nq),
            in_specs=[pl.BlockSpec((1, 1, 512, 256), lambda v, p: (v, p, 0, 0))],
            out_specs=pl.BlockSpec((1, chans, h, ext, ext), lambda v, p: (v, 0, p, 0, 0)),
            out_shape=jax.ShapeDtypeStruct(x.shape, BF16),
            name="unpack",
        )(dense)

    return jax.shard_map(local, mesh=mesh, in_specs=(spec, P(), P(), P()), out_specs=spec, check_vma=False)
```

time: 749 us -> 69.6 us (0.09)
  the two profiles are of different devices: /device:TPU:97 before, /device:TPU:98 now
where the time goes in v1:
time: 69.6 us; the launch traced here: 69.3 us
  Pallas kernels  64.8 us (93%)
  local copies, waits for them, and re-layouts  4.46 us (6%)
    pallas_call x1, Pallas kernels, local(): pl.pallas_call(functools.partial(kernel, cfg), out_shape=jax.ShapeDtypeSt...  56.5 us
    pallas_call x1, Pallas kernels, local(): pl.pallas_call(unpack_kernel, grid=(vols, nq), in_specs=[pl.BlockSpec((1,...  8.28 us

profile of v1, /device:TPU:98, one launch (start us, length us, event | category | flops | bytes accessed | tf_op | source)
XLA Modules:
  0.0 69.3 jit_solution(16356421336115570950)
XLA Ops:
  0.0 1.4 %reshape.3.taps = f32[153]{0:T(256)} reshape(f32[3,3,17]{2,1,0:T(4,128)} %param.5) | data formatting | bytes 1224 | tf_op jit(solution)/shard_map/reshape | solution.py:331
  1.4 1.4 %copy.6 = bf16[3,16,16]{1,2,0:T(8,128)(2,1)} copy(bf16[3,16,16]{2,1,0:T(8,128)(2,1)} %param.6) | data formatting | bytes 3072 | tf_op args[2]
  2.7 0.8 %broadcast_in_dim.3 = f32[3,16,16]{2,1,0:T(8,128)S(1)} broadcast(f32[3,16]{1,0:T(4,128)} %param.7), dimensions={0,1} | broadcast | bytes 3264 | tf_op jit(solution)/shard_map/broadcast_in_dim | solution.py:288
  3.5 1.0 %broadcast_in_dim_reshape.4.bias = f32[3,256,1]{2,1,0:T(8,128)} reshape(f32[3,16,16]{2,1,0:T(8,128)S(1)} %broadcast_in_dim.3) | data formatting | bytes 6144 | tf_op jit(solution)/shard_map/broadcast_in_dim;reshape | solution.py:288
  4.5 56.5 %layers.1.x_ref = bf16[2,4,512,256]{3,2,1,0:T(8,128)(2,1)} custom-call(bf16[2,16,32,32,32]{4,3,2,1,0:T(8,128)(2,1)} %x_hbm.1, f32[153]{0:T(256)} %reshape.3.taps, bf16[3,16,16]{2,1,0:T(8,128)(2,1)} %bitcast.1, f32[3,256,1]{2,1,0:T(8,128)} %broadcast_in_dim_reshape.4.bias), custom_call_target="tpu_custom_call" | custom-call | tf_op jit(solution)/shard_map/layers/pallas_call | solution.py:290
  61.0 8.3 %unpack.1 = bf16[2,16,32,32,32]{4,3,2,1,0:T(8,128)(2,1)} custom-call(bf16[2,4,512,256]{3,2,1,0:T(8,128)(2,1)} %layers.1.x_ref), custom_call_target="tpu_custom_call" | custom-call | tf_op jit(solution)/shard_map/unpack/pallas_call | solution.py:332

commit v2 on v1

v2 whole, which is shorter than its diff:
```python
import functools
import math

import jax
import jax.numpy as jnp
from jax import lax
from jax.experimental import pallas as pl
from jax.experimental.pallas import tpu as pltpu
from jax.sharding import PartitionSpec as P

MESH = pl.DeviceIdType.MESH
F32 = jnp.float32
BF16 = jnp.bfloat16
LAG_B = 3
LAG_C = 7


def dot(a, b):
    return jnp.dot(a, b, preferred_element_type=F32)


def iota2(shape, dim):
    return lax.broadcasted_iota(jnp.int32, shape, dim)


def kernel(cfg, x_hbm, taps_hbm, weight_hbm, bias_hbm, out_ref, taps, weight, bias, stage, vb, u1, u2, jsend, jlo, jhi, ksend, klo, khi,
           mi, mj, mjh, mk, mkh, mw, ms, bcol, arg_sem, in_sem, xs_sem, xr_sem, js_sem, jr_sem, ks_sem, kr_sem):
    layers, vols, nq, chans, ext, h, ktaps, ny, nz = cfg
    per_layer = vols * nq
    total = layers * per_layer
    px, py, pz = lax.axis_index("px"), lax.axis_index("py"), lax.axis_index("pz")
    mate = 1 - px
    y_lo, y_hi, z_lo, z_hi = py > 0, py < ny - 1, pz > 0, pz < nz - 1

    def place(q):
        return px * q + (1 - px) * (nq - 1 - q)

    def index(n):
        return n // per_layer, (n // nq) % vols, n % nq

    def in_copy(c):
        v, q = c // nq, c % nq
        return pltpu.make_async_copy(x_hbm.at[v, :, pl.ds(place(q) * h, h)], stage.at[c], in_sem.at[c])

    def x_copy(l, v):
        src = px * 1 + (1 - px) * nq
        dst = px * (nq + 1)
        return pltpu.make_async_remote_copy(vb.at[l, v, src], vb.at[l, v, dst], xs_sem.at[l, v], xr_sem.at[l, v],
                                            device_id={"px": mate}, device_id_type=MESH)

    def j_copies(n):
        return (
            (y_hi, y_lo, pltpu.make_async_remote_copy(jsend.at[n, 1], jlo.at[n], js_sem.at[n, 1], jr_sem.at[n, 0],
                                                      device_id={"py": py + 1}, device_id_type=MESH)),
            (y_lo, y_hi, pltpu.make_async_remote_copy(jsend.at[n, 0], jhi.at[n], js_sem.at[n, 0], jr_sem.at[n, 1],
                                                      device_id={"py": py - 1}, device_id_type=MESH)),
        )

    def k_copies(n):
        return (
            (z_hi, z_lo, pltpu.make_async_remote_copy(ksend.at[n, 1], klo.at[n], ks_sem.at[n, 1], kr_sem.at[n, 0],
                                                      device_id={"pz": pz + 1}, device_id_type=MESH)),
            (z_lo, z_hi, pltpu.make_async_remote_copy(ksend.at[n, 0], khi.at[n], ks_sem.at[n, 0], kr_sem.at[n, 1],
                                                      device_id={"pz": pz - 1}, device_id_type=MESH)),
        )

    lanes = iota2((ext, 256), 1)
    rows = iota2((ext, 256), 0)
    lane_i, lane_k = lanes // ext, lanes % ext

    def banded(layer, axis, diff):
        acc = jnp.zeros(diff.shape, F32)
        for t in range(ktaps):
            acc = jnp.where(diff == t, taps[layer, axis, t], acc)
        return acc

    def build_i(layer):
        vals = banded(layer, 0, iota2((3 * h, 256), 0) - iota2((3 * h, 256), 1) // ext)
        for i_in in range(3 * h):
            full = jnp.broadcast_to(vals[i_in:i_in + 1, :], (ext, 256))
            mi[layer, pl.ds(i_in * ext, ext), :] = jnp.where(lane_k == rows, full, 0.0).astype(BF16)

    def build_pack():
        dirn, hh, i8, kk = lanes // 128, (lanes // 64) % 2, (lanes // h) % 8, lanes % h
        for q in range(2):
            for g in range(8):
                hit = (hh == q) & (i8 == g) & (rows == kk + (ext - h) * dirn)
                ms[q, pl.ds(g * ext, ext), :] = jnp.where(hit, 1.0, 0.0).astype(BF16)

    def build_j(layer):
        tj = banded(layer, 1, lane_k - rows + h)
        l2, r2 = lanes[:, :128], rows[:, :128]
        d2, c2, jj = l2 // 64, (l2 // h) % 8, l2 % h
        tjh = banded(layer, 1, jj + d2 * (ext + h) - r2)
        for g in range(8):
            mj[layer, pl.ds(g * ext, ext), :] = jnp.where(lane_i == g, tj, 0.0).astype(BF16)
            mjh[layer, pl.ds(g * ext, ext), :] = jnp.where(c2 == g, tjh, 0.0).astype(BF16)

    def build_k(layer):
        tk = banded(layer, 2, rows - lane_k + h)
        for g in range(8):
            mk[layer, pl.ds(g * ext, ext), :] = jnp.where(lane_i == g, tk, 0.0).astype(BF16)
        l3, r3 = lanes[:16, :], rows[:16, :]
        zero = jnp.zeros((64, 256), BF16)
        for d in range(2):
            tkh = banded(layer, 2, r3 % h + d * (ext + h) - l3 % ext)
            for half in range(2):
                mkh[layer, 1 - half, pl.ds(d * 128 + half * 64, 64), :] = zero
                for g in range(0, 8, 2):
                    part = jnp.where(l3 // ext == g + r3 // h, tkh, 0.0).astype(BF16)
                    mkh[layer, half, pl.ds(d * 128 + half * 64 + g * h, 16), :] = part

    def build_mix(layer):
        e_rows = jnp.where(iota2((256, 16), 0) // 16 == iota2((256, 16), 1), 1.0, 0.0).astype(BF16)
        e_cols = jnp.where(iota2((16, 256), 1) // 16 == iota2((16, 256), 0), 1.0, 0.0).astype(BF16)
        tall = lax.dot_general(e_rows, weight[layer], (((1,), (1,)), ((), ())), preferred_element_type=F32)
        wide = dot(tall.astype(BF16), e_cols)
        mw[layer] = jnp.where(iota2((256, 256), 0) % 16 == iota2((256, 256), 1) % 16, wide, 0.0).astype(BF16)
        for d in range(chans):
            bcol[layer, pl.ds(d * 16, 16), :] = jnp.full((16, 128), bias[layer, d], F32)

    def convert(c):
        v, q = c // nq, c % nq
        in_copy(c).wait()
        parts = [stage[c, :, a].reshape(chans * ext, ext) for a in range(h)]
        vb[0, v, place(q) + 1] = jnp.concatenate(parts, axis=1)

    def when(cond, do):
        if isinstance(cond, bool):
            if cond:
                do()
        else:
            pl.when(cond)(do)

    def wait_x(n):
        l, v, q = index(n)
        when(q == 0, lambda: x_copy(l, v).wait_recv())

    def wait_all(copies):
        for _, here, copy in copies:
            pl.when(here)(copy.wait_recv)

    def start_all(copies):
        for there, _, copy in copies:
            pl.when(there)(copy.start)

    def compute_b(n):
        l, v, q = index(n)
        n_lo = jnp.where(y_lo, n, total)
        n_hi = jnp.where(y_hi, n, total)
        packed = None
        for half in range(2):
            main = u1[n % 4, pl.ds(half * 256, 256), :]
            halo = jnp.concatenate([jlo[n_lo, pl.ds(half * 64, 64), :], jhi[n_hi, pl.ds(half * 64, 64), :]], axis=0)
            acc = (dot(mj[l], main) + dot(mjh[l], halo)).astype(BF16)
            u2[n % 4, pl.ds(half * 256, 256), :] = acc
            term = dot(acc, ms[half])
            packed = term if packed is None else packed + term
        packed = packed.astype(BF16)
        ksend[n, 0] = packed[:, :128]
        ksend[n, 1] = packed[:, 128:]

    def compute_a(n):
        l, v, q = index(n)
        s = place(q) + 1
        acc = dot(vb[l, v, s - 1], mi[l, 0:256]) + dot(vb[l, v, s], mi[l, 256:512]) + dot(vb[l, v, s + 1], mi[l, 512:768])
        u1[n % 4] = acc.astype(BF16)
        cut = acc.reshape(chans, ext // h, h, 256)
        jsend[n, 0] = cut[:, 0].reshape(chans * h, 256).astype(BF16)
        jsend[n, 1] = cut[:, ext // h - 1].reshape(chans * h, 256).astype(BF16)

    def compute_c(n, store):
        l, v, q = index(n)
        n_lo = jnp.where(z_lo, n, total)
        n_hi = jnp.where(z_hi, n, total)
        halo = jnp.concatenate([klo[n_lo], khi[n_hi]], axis=1)
        u3 = []
        for half in range(2):
            acc = dot(u2[n % 4, pl.ds(half * 256, 256), :], mk[l]) + dot(halo, mkh[l, half])
            u3.append(acc.astype(BF16).reshape(8, 2, 16, 256))
        s = place(q) + 1
        b128 = bcol[l]
        shift = jnp.concatenate([b128, b128], axis=1)
        old = vb[l, v, s].reshape(chans, 2, 16, 256)
        new = []
        for jh in range(2):
            rhs = jnp.concatenate([u3[0][:, jh].reshape(128, 256), u3[1][:, jh].reshape(128, 256)], axis=0)
            z = dot(mw[l], rhs) + shift
            inner = z * (math.sqrt(2.0 / math.pi) + (0.044715 * math.sqrt(2.0 / math.pi)) * (z * z))
            half_z = 0.5 * z
            act = half_z + half_z * jnp.tanh(inner)
            res = old[:, jh].reshape(256, 256).astype(F32) + act
            new.append(res.astype(BF16).reshape(chans, 1, 16, 256))
        store(n, jnp.concatenate(new, axis=1).reshape(512, 256))

    def store_state(n, result):
        l, v, q = index(n)
        vb[l + 1, v, place(q) + 1] = result

    def store_out(n, result):
        l, v, q = index(n)
        out_ref[v, place(q)] = result

    def tick(a, b, c, last):
        if c is not None:
            wait_all(k_copies(c))
            compute_c(c, store_out if last else store_state)
            l, v, q = index(c)
            if not last:
                when(q == 0, lambda: x_copy(l + 1, v).start())
        if b is not None:
            wait_all(j_copies(b))
        if a is not None:
            wait_x(a)
        if b is not None:
            compute_b(b)
        if a is not None:
            compute_a(a)
        if b is not None:
            start_all(k_copies(b))
        if a is not None:
            start_all(j_copies(a))

    arg_copies = [pltpu.make_async_copy(taps_hbm, taps, arg_sem.at[0]),
                  pltpu.make_async_copy(weight_hbm, weight, arg_sem.at[1]),
                  pltpu.make_async_copy(bias_hbm, bias, arg_sem.at[2])]
    for copy in arg_copies:
        copy.start()
    for c in range(3):
        in_copy(c).start()
    barrier = pltpu.get_barrier_semaphore()
    pl.semaphore_signal(barrier, inc=1, device_id={"px": mate}, device_id_type=MESH)
    for cond, name, other in ((y_lo, "py", py - 1), (y_hi, "py", py + 1), (z_lo, "pz", pz - 1), (z_hi, "pz", pz + 1)):
        @pl.when(cond)
        def _(name=name, other=other):
            pl.semaphore_signal(barrier, inc=1, device_id={name: other}, device_id_type=MESH)

    for copy in arg_copies:
        copy.wait()
    build_i(0)
    edge_slot = px * (nq + 1)
    big_zero = jnp.zeros((512, 256), BF16)
    for l in range(layers):
        for v in range(vols):
            vb[l, v, edge_slot] = big_zero
    jlo[total] = jnp.zeros((128, 256), BF16)
    jhi[total] = jnp.zeros((128, 256), BF16)
    klo[total] = jnp.zeros((256, 128), BF16)
    khi[total] = jnp.zeros((256, 128), BF16)

    convert(0)
    n_wait = 1 + y_lo.astype(jnp.int32) + y_hi.astype(jnp.int32) + z_lo.astype(jnp.int32) + z_hi.astype(jnp.int32)
    pl.semaphore_wait(barrier, n_wait)
    x_copy(0, 0).start()
    for c in range(3, per_layer):
        in_copy(c).start()
    convert(1)

    for t in range(LAG_C):
        tick(t, t - LAG_B if t >= LAG_B else None, None, False)
        if t + 2 < per_layer:
            convert(t + 2)
            if (t + 2) % nq == 0:
                x_copy(0, (t + 2) // nq).start()
        if t == 0:
            build_j(0)
            build_pack()
        elif t == 1:
            build_k(0)
        elif t == 2:
            build_mix(0)
        elif t == 3:
            for l in range(1, layers):
                build_i(l)
        elif t == 4:
            for l in range(1, layers):
                build_j(l)
        elif t == 5:
            for l in range(1, layers):
                build_k(l)
                build_mix(l)

    split = per_layer * (layers - 1)

    def steady(t, _):
        tick(t, t - LAG_B, t - LAG_C, False)
        return 0

    lax.fori_loop(LAG_C, split + LAG_C, steady, 0)
    for t in range(split + LAG_C, total + LAG_C):
        tick(t if t < total else None, t - LAG_B if t < total + LAG_B else None, t - LAG_C, True)

    def drain(n, _):
        for there, _, copy in j_copies(n) + k_copies(n):
            pl.when(there)(copy.wait_send)
        return 0

    lax.fori_loop(0, total, drain, 0)
    for l in range(layers):
        for v in range(vols):
            x_copy(l, v).wait_send()


def unpack_kernel(nq, dense, o_hbm, stage, out_sem):
    vols, _, rows, width = dense.shape
    chans, h, ext = stage.shape[1:4]
    count = vols * nq
    outs = [pltpu.make_async_copy(stage.at[c], o_hbm.at[c // nq, :, pl.ds((c % nq) * h, h)], out_sem.at[c]) for c in range(count)]
    for c in range(count):
        for group in range(width // 128):
            block = dense[c // nq, c % nq, :, group * 128:(group + 1) * 128]
            for a in range(128 // ext):
                moved = block if a == 0 else pltpu.roll(block, 128 - ext * a, 1)
                stage[c, :, group * (128 // ext) + a] = moved[:, :ext].reshape(chans, ext, ext)
        outs[c].start()
    for copy in outs:
        copy.wait()


def solution(mesh):
    ny, nz = mesh.shape["py"], mesh.shape["pz"]
    spec = P("dp", None, "px", "py", "pz")

    def local(x, filter_taps, mix_weight, mix_bias):
        vols, chans, ext = x.shape[0], x.shape[1], x.shape[2]
        layers, ktaps = filter_taps.shape[0], filter_taps.shape[2]
        h = (ktaps - 1) // 2
        nq = ext // h
        total = layers * vols * nq
        cfg = (layers, vols, nq, chans, ext, h, ktaps, ny, nz)
        dense = pl.pallas_call(
            functools.partial(kernel, cfg),
            out_shape=jax.ShapeDtypeStruct((vols, nq, 512, 256), BF16),
            in_specs=[pl.BlockSpec(memory_space=pltpu.HBM)] * 4,
            out_specs=pl.BlockSpec(memory_space=pltpu.VMEM),
            scratch_shapes=[
                pltpu.SMEM(filter_taps.shape, F32),
                pltpu.VMEM(mix_weight.shape, BF16),
                pltpu.SMEM(mix_bias.shape, F32),
                pltpu.VMEM((vols * nq, chans, h, ext, ext), BF16),
                pltpu.VMEM((layers, vols, nq + 2, 512, 256), BF16),
                pltpu.VMEM((4, 512, 256), BF16),
                pltpu.VMEM((4, 512, 256), BF16),
                pltpu.VMEM((total, 2, 128, 256), BF16),
                pltpu.VMEM((total + 1, 128, 256), BF16),
                pltpu.VMEM((total + 1, 128, 256), BF16),
                pltpu.VMEM((total, 2, 256, 128), BF16),
                pltpu.VMEM((total + 1, 256, 128), BF16),
                pltpu.VMEM((total + 1, 256, 128), BF16),
                pltpu.VMEM((layers, 768, 256), BF16),
                pltpu.VMEM((layers, 256, 256), BF16),
                pltpu.VMEM((layers, 256, 128), BF16),
                pltpu.VMEM((layers, 256, 256), BF16),
                pltpu.VMEM((layers, 2, 256, 256), BF16),
                pltpu.VMEM((layers, 256, 256), BF16),
                pltpu.VMEM((2, 256, 256), BF16),
                pltpu.VMEM((layers, 256, 128), F32),
                pltpu.SemaphoreType.DMA((3,)),
                pltpu.SemaphoreType.DMA((vols * nq,)),
                pltpu.SemaphoreType.DMA((layers, vols)),
                pltpu.SemaphoreType.DMA((layers, vols)),
                pltpu.SemaphoreType.DMA((total, 2)),
                pltpu.SemaphoreType.DMA((total, 2)),
                pltpu.SemaphoreType.DMA((total, 2)),
                pltpu.SemaphoreType.DMA((total, 2)),
            ],
            compiler_params=pltpu.CompilerParams(collective_id=0, has_side_effects=True, vmem_limit_bytes=50 * 1024 * 1024),
            name="layers",
        )(x, filter_taps, mix_weight, mix_bias)
        return pl.pallas_call(
            functools.partial(unpack_kernel, nq),
            in_specs=[pl.BlockSpec(memory_space=pltpu.VMEM)],
            out_specs=pl.BlockSpec(memory_space=pl.ANY),
            out_shape=jax.ShapeDtypeStruct(x.shape, BF16),
            scratch_shapes=[
                pltpu.VMEM((vols * nq, chans, h, ext, ext), BF16),
                pltpu.SemaphoreType.DMA((vols * nq,)),
            ],
            compiler_params=pltpu.CompilerParams(vmem_limit_bytes=32 * 1024 * 1024),
            name="unpack",
        )(dense)

    return jax.shard_map(local, mesh=mesh, in_specs=(spec, P(), P(), P()), out_specs=spec, check_vma=False)
```

time: 69.6 us -> 55.8 us (0.80)
  the two profiles are of different devices: /device:TPU:98 before, /device:TPU:97 now
where the time goes in v2:
time: 55.8 us; the launch traced here: 55.6 us
  Pallas kernels  53.4 us (96%)
  local copies, waits for them, and re-layouts  2.08 us (4%)
    pallas_call x1, Pallas kernels, local(): pl.pallas_call(functools.partial(kernel, cfg), out_shape=jax.ShapeDtypeSt...  49.7 us
    pallas_call x1, Pallas kernels, local(): pl.pallas_call(functools.partial(unpack_kernel, nq), in_specs=[pl.BlockSp...  3.64 us
    unnamed x6, local copies, waits for them, and re-layouts  2.08 us

profile of v2, /device:TPU:97, one launch (start us, length us, event | category | flops | bytes accessed | tf_op | source)
XLA Modules:
  0.0 55.6 jit_solution(2169275705372147606)
XLA Ops:
  0.0 0.0 copy-start
  0.0 0.7 %copy-done = bf16[3,16,16]{2,1,0:T(8,128)(2,1)S(1)} copy-done((bf16[3,16,16]{2,1,0:T(8,128)(2,1)S(1)}, bf16[3,16,16]{2,1,0:T(8,128)(2,1)}, u32[]{:S(2)}) %copy-start) | copy-done | bytes 1560
  0.7 0.0 copy-start.1
  0.7 0.7 %copy-done.1 = f32[3,3,17]{2,1,0:T(4,128)S(1)} copy-done((f32[3,3,17]{2,1,0:T(4,128)S(1)}, f32[3,3,17]{2,1,0:T(4,128)}, u32[]{:S(2)}) %copy-start.1) | copy-done | bytes 636
  1.4 0.0 copy-start.2
  1.4 0.7 %copy-done.2 = f32[3,16]{1,0:T(4,128)S(1)} copy-done((f32[3,16]{1,0:T(4,128)S(1)}, f32[3,16]{1,0:T(4,128)}, u32[]{:S(2)}) %copy-start.2) | copy-done | bytes 216
  2.1 49.7 %layers.1.dense = bf16[2,4,512,256]{3,2,1,0:T(8,128)(2,1)S(1)} custom-call(bf16[2,16,32,32,32]{4,3,2,1,0:T(8,128)(2,1)} %x_hbm.1, f32[3,3,17]{2,1,0:T(4,128)S(1)} %copy-done.1, bf16[3,16,16]{2,1,0:T(8,128)(2,1)S(1)} %copy-done, f32[3,16]{1,0:T(4,128)S(1)} %copy-done.2), custom_call_target="tpu_custom_call" | custom-call | tf_op jit(solution)/shard_map/layers/pallas_call | solution.py:331
  51.8 3.6 %unpack.1 = bf16[2,16,32,32,32]{4,3,2,1,0:T(8,128)(2,1)} custom-call(bf16[2,4,512,256]{3,2,1,0:T(8,128)(2,1)S(1)} %layers.1.dense), custom_call_target="tpu_custom_call" | custom-call | tf_op jit(solution)/shard_map/unpack/pallas_call | solution.py:370
Async XLA Ops:
  0.0 0.7 %copy-start = (bf16[3,16,16]{2,1,0:T(8,128)(2,1)S(1)}, bf16[3,16,16]{2,1,0:T(8,128)(2,1)}, u32[]{:S(2)}) copy-start(bf16[3,16,16]{2,1,0:T(8,128)(2,1)} %weight_hbm.1) | copy-start | bytes 4612
  0.7 0.7 %copy-start.1 = (f32[3,3,17]{2,1,0:T(4,128)S(1)}, f32[3,3,17]{2,1,0:T(4,128)}, u32[]{:S(2)}) copy-start(f32[3,3,17]{2,1,0:T(4,128)} %taps_hbm.1) | copy-start | bytes 1840
  1.4 0.7 %copy-start.2 = (f32[3,16]{1,0:T(4,128)S(1)}, f32[3,16]{1,0:T(4,128)}, u32[]{:S(2)}) copy-start(f32[3,16]{1,0:T(4,128)} %bias_hbm.1) | copy-start | bytes 580

commit v3 on v2

--- a/solution.py
+++ b/solution.py
@@ -366,7 +366,7 @@
             ],
             compiler_params=pltpu.CompilerParams(collective_id=0, has_side_effects=True, vmem_limit_bytes=50 * 1024 * 1024),
             name="layers",
-        )(x, filter_taps, mix_weight, mix_bias)
+        )(x, *(pltpu.with_memory_space_constraint(a, pltpu.HBM) for a in (filter_taps, mix_weight, mix_bias)))
         return pl.pallas_call(
             functools.partial(unpack_kernel, nq),
             in_specs=[pl.BlockSpec(memory_space=pltpu.VMEM)],

time: 55.8 us -> 53.6 us (0.961)
  local copies, waits for them, and re-layouts: 2.08 us -> 0 us
    unnamed x6 -> x0, local copies, waits for them, and re-layouts: 2.08 us -> none
where the time goes in v3:
time: 53.6 us; the launch traced here: 53.5 us
  Pallas kernels  53.4 us (100%)
    pallas_call x1, Pallas kernels, local(): pl.pallas_call(functools.partial(kernel, cfg), out_shape=jax.ShapeDtypeSt...  49.7 us
    pallas_call x1, Pallas kernels, local(): pl.pallas_call(functools.partial(unpack_kernel, nq), in_specs=[pl.BlockSp...  3.64 us

profile of v3, /device:TPU:97, one launch (start us, length us, event | category | flops | bytes accessed | tf_op | source)
XLA Modules:
  0.0 53.5 jit_solution(2851305264482963319)
XLA Ops:
  0.0 49.7 %layers.1.dense = bf16[2,4,512,256]{3,2,1,0:T(8,128)(2,1)S(1)} custom-call(bf16[2,16,32,32,32]{4,3,2,1,0:T(8,128)(2,1)} %x_hbm.1, f32[3,3,17]{2,1,0:T(4,128)} %taps_hbm.1, bf16[3,16,16]{2,1,0:T(8,128)(2,1)} %weight_hbm.1, f32[3,16]{1,0:T(4,128)} %bias_hbm.1), custom_call_target="tpu_custom_call" | custom-call | tf_op jit(solution)/shard_map/layers/pallas_call | solution.py:331
  49.7 3.6 %unpack.1 = bf16[2,16,32,32,32]{4,3,2,1,0:T(8,128)(2,1)} custom-call(bf16[2,4,512,256]{3,2,1,0:T(8,128)(2,1)S(1)} %layers.1.dense), custom_call_target="tpu_custom_call" | custom-call | tf_op jit(solution)/shard_map/unpack/pallas_call | solution.py:370

commit v4 on v3

--- a/solution.py
+++ b/solution.py
@@ -216,18 +216,17 @@
             compute_b(b)
         if a is not None:
             compute_a(a)
+        if a is not None:
+            start_all(j_copies(a))
         if b is not None:
             start_all(k_copies(b))
-        if a is not None:
-            start_all(j_copies(a))
 
     arg_copies = [pltpu.make_async_copy(taps_hbm, taps, arg_sem.at[0]),
                   pltpu.make_async_copy(weight_hbm, weight, arg_sem.at[1]),
                   pltpu.make_async_copy(bias_hbm, bias, arg_sem.at[2])]
+    in_copy(0).start()
     for copy in arg_copies:
         copy.start()
-    for c in range(3):
-        in_copy(c).start()
     barrier = pltpu.get_barrier_semaphore()
     pl.semaphore_signal(barrier, inc=1, device_id={"px": mate}, device_id_type=MESH)
     for cond, name, other in ((y_lo, "py", py - 1), (y_hi, "py", py + 1), (z_lo, "pz", pz - 1), (z_hi, "pz", pz + 1)):
@@ -235,9 +234,6 @@
         def _(name=name, other=other):
             pl.semaphore_signal(barrier, inc=1, device_id={name: other}, device_id_type=MESH)
 
-    for copy in arg_copies:
-        copy.wait()
-    build_i(0)
     edge_slot = px * (nq + 1)
     big_zero = jnp.zeros((512, 256), BF16)
     for l in range(layers):
@@ -248,12 +244,16 @@
     klo[total] = jnp.zeros((256, 128), BF16)
     khi[total] = jnp.zeros((256, 128), BF16)
 
+    in_copy(1).start()
     convert(0)
     n_wait = 1 + y_lo.astype(jnp.int32) + y_hi.astype(jnp.int32) + z_lo.astype(jnp.int32) + z_hi.astype(jnp.int32)
     pl.semaphore_wait(barrier, n_wait)
     x_copy(0, 0).start()
-    for c in range(3, per_layer):
+    for c in range(2, per_layer):
         in_copy(c).start()
+    for copy in arg_copies:
+        copy.wait()
+    build_i(0)
     convert(1)
 
     for t in range(LAG_C):
@@ -262,12 +262,11 @@
             convert(t + 2)
             if (t + 2) % nq == 0:
                 x_copy(0, (t + 2) // nq).start()
-        if t == 0:
+        if t == 1:
             build_j(0)
             build_pack()
-        elif t == 1:
+        elif t == 2:
             build_k(0)
-        elif t == 2:
             build_mix(0)
         elif t == 3:
             for l in range(1, layers):
@@ -278,6 +277,8 @@
         elif t == 5:
             for l in range(1, layers):
                 build_k(l)
+        elif t == 6:
+            for l in range(1, layers):
                 build_mix(l)
 
     split = per_layer * (layers - 1)
@@ -304,15 +305,17 @@
 def unpack_kernel(nq, dense, o_hbm, stage, out_sem):
     vols, _, rows, width = dense.shape
     chans, h, ext = stage.shape[1:4]
-    count = vols * nq
-    outs = [pltpu.make_async_copy(stage.at[c], o_hbm.at[c // nq, :, pl.ds((c % nq) * h, h)], out_sem.at[c]) for c in range(count)]
-    for c in range(count):
-        for group in range(width // 128):
+    groups, span = width // 128, 128 // ext
+    outs = []
+    for c in range(vols * nq):
+        for group in range(groups):
             block = dense[c // nq, c % nq, :, group * 128:(group + 1) * 128]
-            for a in range(128 // ext):
+            for a in range(span):
                 moved = block if a == 0 else pltpu.roll(block, 128 - ext * a, 1)
-                stage[c, :, group * (128 // ext) + a] = moved[:, :ext].reshape(chans, ext, ext)
-        outs[c].start()
+                stage[c, :, group * span + a] = moved[:, :ext].reshape(chans, ext, ext)
+            outs.append(pltpu.make_async_copy(stage.at[c, :, pl.ds(group * span, span)],
+                                              o_hbm.at[c // nq, :, pl.ds((c % nq) * h + group * span, span)], out_sem.at[c, group]))
+            outs[-1].start()
     for copy in outs:
         copy.wait()
 
@@ -374,7 +377,7 @@
             out_shape=jax.ShapeDtypeStruct(x.shape, BF16),
             scratch_shapes=[
                 pltpu.VMEM((vols * nq, chans, h, ext, ext), BF16),
-                pltpu.SemaphoreType.DMA((vols * nq,)),
+                pltpu.SemaphoreType.DMA((vols * nq, 2)),
             ],
             compiler_params=pltpu.CompilerParams(vmem_limit_bytes=32 * 1024 * 1024),
             name="unpack",

time: 53.6 us -> 53.5 us (level)
  no operation moved by 1% of the time
where the time goes in v4:
time: 53.5 us; the launch traced here: 53.4 us
  Pallas kernels  53.2 us (99%)
    pallas_call x1, Pallas kernels, local(): pl.pallas_call(functools.partial(kernel, cfg), out_shape=jax.ShapeDtypeSt...  49.6 us
    pallas_call x1, Pallas kernels, local(): pl.pallas_call(functools.partial(unpack_kernel, nq), in_specs=[pl.BlockSp...  3.58 us

profile of v4, /device:TPU:97, one launch (start us, length us, event | category | flops | bytes accessed | tf_op | source)
XLA Modules:
  0.0 53.4 jit_solution(10499740848171709132)
XLA Ops:
  0.0 49.6 %layers.1.dense = bf16[2,4,512,256]{3,2,1,0:T(8,128)(2,1)S(1)} custom-call(bf16[2,16,32,32,32]{4,3,2,1,0:T(8,128)(2,1)} %x_hbm.1, f32[3,3,17]{2,1,0:T(4,128)} %taps_hbm.1, bf16[3,16,16]{2,1,0:T(8,128)(2,1)} %weight_hbm.1, f32[3,16]{1,0:T(4,128)} %bias_hbm.1), custom_call_target="tpu_custom_call" | custom-call | tf_op jit(solution)/shard_map/layers/pallas_call | solution.py:334
  49.6 3.6 %unpack.1 = bf16[2,16,32,32,32]{4,3,2,1,0:T(8,128)(2,1)} custom-call(bf16[2,4,512,256]{3,2,1,0:T(8,128)(2,1)S(1)} %layers.1.dense), custom_call_target="tpu_custom_call" | custom-call | tf_op jit(solution)/shard_map/unpack/pallas_call | solution.py:373

commit v5 on v4

--- a/solution.py
+++ b/solution.py
@@ -288,18 +288,20 @@
         return 0
 
     lax.fori_loop(LAG_C, split + LAG_C, steady, 0)
-    for t in range(split + LAG_C, total + LAG_C):
-        tick(t if t < total else None, t - LAG_B if t < total + LAG_B else None, t - LAG_C, True)
-
     def drain(n, _):
         for there, _, copy in j_copies(n) + k_copies(n):
             pl.when(there)(copy.wait_send)
         return 0
 
-    lax.fori_loop(0, total, drain, 0)
-    for l in range(layers):
-        for v in range(vols):
-            x_copy(l, v).wait_send()
+    for t in range(split + LAG_C, total + LAG_C):
+        if t == total + LAG_C - 1:
+            lax.fori_loop(0, total - 2, drain, 0)
+            for l in range(layers):
+                for v in range(vols):
+                    x_copy(l, v).wait_send()
+        tick(t if t < total else None, t - LAG_B if t < total + LAG_B else None, t - LAG_C, True)
+
+    lax.fori_loop(total - 2, total, drain, 0)
 
 
 def unpack_kernel(nq, dense, o_hbm, stage, out_sem):

time: 53.5 us -> 53.4 us (level)
  no operation moved by 1% of the time
where the time goes in v5:
time: 53.4 us; the launch traced here: 53.1 us
  Pallas kernels  52.9 us (99%)
    pallas_call x1, Pallas kernels, local(): pl.pallas_call(functools.partial(kernel, cfg), out_shape=jax.ShapeDtypeSt...  49.3 us
    pallas_call x1, Pallas kernels, local(): pl.pallas_call(functools.partial(unpack_kernel, nq), in_specs=[pl.BlockSp...  3.58 us

profile of v5, /device:TPU:97, one launch (start us, length us, event | category | flops | bytes accessed | tf_op | source)
XLA Modules:
  0.0 53.1 jit_solution(5202788713768374180)
XLA Ops:
  0.0 49.3 %layers.1.dense = bf16[2,4,512,256]{3,2,1,0:T(8,128)(2,1)S(1)} custom-call(bf16[2,16,32,32,32]{4,3,2,1,0:T(8,128)(2,1)} %x_hbm.1, f32[3,3,17]{2,1,0:T(4,128)} %taps_hbm.1, bf16[3,16,16]{2,1,0:T(8,128)(2,1)} %weight_hbm.1, f32[3,16]{1,0:T(4,128)} %bias_hbm.1), custom_call_target="tpu_custom_call" | custom-call | tf_op jit(solution)/shard_map/layers/pallas_call | solution.py:336
  49.3 3.6 %unpack.1 = bf16[2,16,32,32,32]{4,3,2,1,0:T(8,128)(2,1)} custom-call(bf16[2,4,512,256]{3,2,1,0:T(8,128)(2,1)S(1)} %layers.1.dense), custom_call_target="tpu_custom_call" | custom-call | tf_op jit(solution)/shard_map/unpack/pallas_call | solution.py:375
